TPU v7x, 32 devices: a whole 2x2x4 slice. The times are simulated.
32 devices in a mesh: curve: 8 (over z, y), sub: 4 (over x, core).
Axes of the slice: x: 2, y: 2, z: 4, core: 2. Of those that a mesh axis runs over, the one named last changes fastest.
Arguments:
- forcing: float32 [12, 768, 1024], P(None, 'curve', 'sub'), may hold values from -10 to 10
- metric: float32 [768, 1024], P('curve', 'sub'), may hold values from 0.25 to 4
- jacobian: float32 [768, 1024], P('curve', 'sub'), may hold values from 0.5 to 2
- mode_scale: float32 [12], replicated, may hold values from 0.1 to 10
Outputs:
- solution: float32 [12, 768, 1024], P(None, 'curve', 'sub')
- residual: float32 [12, 768, 1024], P(None, 'curve', 'sub')
All inputs are finite; a program needn't handle non-finite values.
Results may differ from a plain program's by a relative error of at most 0.0003.
Values sent between devices are 32-bit elements; how exact they have to be, the bound alone decides.
A program may use at most 64 MiB of HBM per device.

v0:
```python
import functools
import math

import jax
import jax.numpy as jnp
import numpy as np
from jax import lax
from jax.experimental import pallas as pl
from jax.experimental.pallas import tpu as pltpu
from jax.sharding import PartitionSpec as P

ITERS = 3
MESH = pl.DeviceIdType.MESH
LANES = 128
f32 = jnp.float32
bf16 = jnp.bfloat16


def gll_tables():
    points = np.array([-1.0, -1.0 / math.sqrt(5.0), 1.0 / math.sqrt(5.0), 1.0])
    weights = np.array([1.0 / 6.0, 5.0 / 6.0, 5.0 / 6.0, 1.0 / 6.0])
    factor = np.array(
        [np.prod([points[j] - points[m] for m in range(4) if m != j]) for j in range(4)]
    )
    slopes = np.zeros((4, 4))
    for i in range(4):
        for j in range(4):
            if i != j:
                slopes[i, j] = factor[i] / (factor[j] * (points[i] - points[j]))
        slopes[i, i] = sum((1.0 / (points[i] - points[m]) for m in range(4) if m != i))
    return (slopes, weights)


SLOPES, WEIGHTS = gll_tables()


def combo(coefs, parts):
    total = None
    for c, v in zip(coefs, parts):
        if abs(c) < 1e-12:
            continue
        term = v * f32(c)
        total = term if total is None else total + term
    return total


def kernel(
    nc, ns, modes,
    scale_ref, forcing_ref, metric_ref, jac_ref, grad_ref, div_ref,
    sol_ref, res_ref,
    x, r, z, d, s, w, invp, mass, flux, zcat, gout, sums, coef,
    row_tx, row_rx, col_tx, col_rx, cor_rx, ar_tx, ar_rx,
    source, factors, sol_buf, res_buf,
    htx_sem, hrx_sem, atx_sem, arx_sem, in_sem, out_sem,
):
    rows, cols = metric_ref.shape
    tiles = cols // LANES
    loads = []
    for c in range(tiles):
        cut = pl.ds(c * LANES, LANES)
        loads += [
            pltpu.make_async_copy(jac_ref.at[:, cut], factors.at[0, c], in_sem.at[0, c]),
            pltpu.make_async_copy(metric_ref.at[:, cut], factors.at[1, c], in_sem.at[1, c]),
            pltpu.make_async_copy(forcing_ref.at[:, :, cut], source.at[c], in_sem.at[2, c]),
        ]
    for copy in loads:
        copy.start()
    q = rows // 4
    n = nc * ns
    half = cols - LANES
    me_c, me_s = lax.axis_index("curve"), lax.axis_index("sub")
    me = me_c * ns + me_s
    up, down = lax.rem(me_c + nc - 1, nc), lax.rem(me_c + 1, nc)
    left, right = lax.rem(me_s + ns - 1, ns), lax.rem(me_s + 1, ns)

    def place(offset):
        target = lax.rem(me + offset, n)
        return (target // ns, lax.rem(target, ns))

    barrier = pltpu.get_barrier_semaphore()

    def greet(offset, carry):
        pl.semaphore_signal(barrier, inc=1, device_id=place(offset), device_id_type=MESH)
        return carry

    lax.fori_loop(1, n, greet, 0)

    lane_full = lax.broadcasted_iota(jnp.int32, (q, cols), 1)
    lane = lax.broadcasted_iota(jnp.int32, (q, LANES), 1)
    row_at = lax.broadcasted_iota(jnp.int32, (q, cols), 0)
    phase = lane_full % 4
    on_edge = (phase == 0) | (phase == 3)
    take_next = (phase == 3) & (lane_full != cols - 1)
    take_prev = (phase == 0) & (lane_full != 0)
    half_w = [f32(1.0 / 2.0), f32(1.0), f32(1.0), f32(1.0 / 2.0)]

    def load(ref, m):
        return [ref[m, p * q:(p + 1) * q, :] for p in range(4)]

    def save(ref, m, parts):
        for p in range(4):
            ref[m, p * q:(p + 1) * q, :] = parts[p]

    def load2(ref):
        return [ref[p * q:(p + 1) * q, :] for p in range(4)]

    def pack(rd, m, h, tops):
        lo, hi = tops
        row_tx[rd, 0, pl.ds(m, 1), :] = h[0][0:1, :]
        row_tx[rd, 1, pl.ds(m, 1), :] = h[3][q - 1:q, :]
        t0 = h[0] + jnp.where(row_at == 0, 0.0, pltpu.roll(h[3], 1, 0))
        t3 = h[3] + jnp.where(row_at == q - 1, 0.0, pltpu.roll(h[0], q - 1, 0))
        t = [t0, h[1], h[2], t3]
        save(w, m, t)
        for p in range(4):
            at = 4 * m + p
            lo = jnp.where(lane == at, pltpu.roll(t[p][:, :LANES], at, 1), lo)
            hi = jnp.where(lane == at, pltpu.roll(t[p][:, half:], at + 1, 1), hi)
        return lo, hi

    def halo_copies(rd):
        plan = [
            (row_tx.at[rd, 0], row_rx.at[rd, 1], (up, me_s)),
            (row_tx.at[rd, 1], row_rx.at[rd, 0], (down, me_s)),
            (col_tx.at[rd, 0], col_rx.at[rd, 1], (me_c, left)),
            (col_tx.at[rd, 1], col_rx.at[rd, 0], (me_c, right)),
            (col_tx.at[rd, 0, pl.ds(0, 1)], cor_rx.at[rd, 3], (up, left)),
            (col_tx.at[rd, 1, pl.ds(0, 1)], cor_rx.at[rd, 2], (up, right)),
            (col_tx.at[rd, 0, pl.ds(q - 1, 1)], cor_rx.at[rd, 1], (down, left)),
            (col_tx.at[rd, 1, pl.ds(q - 1, 1)], cor_rx.at[rd, 0], (down, right)),
        ]
        return [
            pltpu.make_async_remote_copy(
                src_ref=src, dst_ref=dst, send_sem=htx_sem.at[rd, k], recv_sem=hrx_sem.at[rd, k],
                device_id=where, device_id_type=MESH)
            for k, (src, dst, where) in enumerate(plan)
        ]

    def finish(rd, count):
        for copy in halo_copies(rd):
            copy.wait_recv()
        ph = lax.broadcasted_iota(jnp.int32, (1, LANES), 1) % 4
        edge_row = lax.broadcasted_iota(jnp.int32, (q, LANES), 0)
        merged = []
        for side in range(2):
            above, below = cor_rx[rd, side], cor_rx[rd, 2 + side]
            above = jnp.where(ph == 0, pltpu.roll(above, LANES - 3, 1), 0.0)
            below = jnp.where(ph == 3, pltpu.roll(below, 3, 1), 0.0)
            c = col_rx[rd, side]
            c = c + jnp.where(edge_row == 0, above, 0.0) + jnp.where(edge_row == q - 1, below, 0.0)
            merged.append(c)

        def body(m, carry):
            t = load(w, m)
            t[0] = t[0] + jnp.where(row_at == 0, row_rx[rd, 0, pl.ds(m, 1), :], 0.0)
            t[3] = t[3] + jnp.where(row_at == q - 1, row_rx[rd, 1, pl.ds(m, 1), :], 0.0)
            for p in range(4):
                at = 4 * m + p
                c = t[p] + jnp.where(
                    take_next, pltpu.roll(t[p], cols - 1, 1),
                    jnp.where(take_prev, pltpu.roll(t[p], 1, 1), 0.0))
                a = jnp.where(lane == 0, pltpu.roll(merged[0], LANES - at, 1), 0.0)
                b = jnp.where(lane == LANES - 1, pltpu.roll(merged[1], LANES - 1 - at, 1), 0.0)
                w[m, p * q:(p + 1) * q, :LANES] = c[:, :LANES] + a
                w[m, p * q:(p + 1) * q, half:] = c[:, half:] + b
            return carry

        lax.fori_loop(0, count, body, 0)

    edge_w, mid_w = f32(1.0 / 6.0), f32(5.0 / 6.0)
    col_w = jnp.where(on_edge, edge_w, mid_w)
    mw, fw = [], []
    for copy in loads:
        copy.wait()
    for p in range(4):
        grid_w = col_w * (edge_w if p in (0, 3) else mid_w)
        mw.append(strided([factors.at[0, c] for c in range(tiles)], p, q) * grid_w)
        fw.append(strided([factors.at[1, c] for c in range(tiles)], p, q) * grid_w)
        mass[p * q:(p + 1) * q, :] = mw[p]
        flux[p * q:(p + 1) * q, :] = fw[p]

    zero = jnp.zeros((q, LANES), f32)

    def start_body(m, carry):
        h = [strided([source.at[c, m] for c in range(tiles)], p, q) * mass[p * q:(p + 1) * q, :] for p in range(4)]
        return pack(0, m, h, carry)

    tops = lax.fori_loop(0, modes, start_body, (zero, zero))
    tops = pack(0, modes, mw, tops)
    table = div_ref[:cols, :].astype(f32) + div_ref[2 * cols:, :].astype(f32)
    by_cols = jnp.dot(flux[...], table * table, precision=lax.Precision.HIGHEST,
                      preferred_element_type=f32)
    squared = SLOPES * SLOPES
    lap = [combo(squared[:, a], fw) + by_cols[a * q:(a + 1) * q, :] for a in range(4)]
    lo, hi = pack(0, modes + 1, lap, tops)
    col_tx[0, 0] = lo
    col_tx[0, 1] = hi

    pl.semaphore_wait(barrier, n - 1)
    for copy in halo_copies(0):
        copy.start()
    finish(0, modes + 2)

    def diag_body(m, carry):
        for p in range(4):
            rs = slice(p * q, (p + 1) * q)
            invp[m, rs, :] = 1.0 / (w[modes, rs, :] + scale_ref[m] * w[modes + 1, rs, :])
            r[m, rs, :] = w[m, rs, :]
        return carry

    lax.fori_loop(0, modes, diag_body, 0)

    pad = (lax.broadcasted_iota(jnp.int32, (1, LANES), 1) >= modes).astype(f32)
    eye = lax.broadcasted_iota(jnp.int32, (16, LANES), 0) == lax.broadcasted_iota(
        jnp.int32, (16, LANES), 1)

    def update(it, m):
        a, b = coef[0, pl.ds(m, 1), :], coef[1, pl.ds(m, 1), :]
        zz, ww = load(z, m), load(w, m)
        if it > 1:
            dd, ss = load(d, m), load(s, m)
            zz = [u + b * v for u, v in zip(zz, dd)]
            ww = [u + b * v for u, v in zip(ww, ss)]
            xx = [u + a * v for u, v in zip(load(x, m), zz)]
        else:
            xx = [a * v for v in zz]
        rr = [u - a * v for u, v in zip(load(r, m), ww)]
        return zz, ww, xx, rr

    def fill(m, parts):
        v = jnp.concatenate(parts, axis=0)
        top = v.astype(bf16)
        at = pl.ds(pl.multiple_of(m * rows, rows), rows)
        zcat[at, :cols] = top
        zcat[at, cols:] = (v - top.astype(f32)).astype(bf16)

    def multiply(table_ref):
        gout[...] = (
            jnp.dot(zcat[...], table_ref[:2 * cols, :], preferred_element_type=f32)
            + jnp.dot(zcat[:, :cols], table_ref[2 * cols:, :], preferred_element_type=f32))

    rho_old = step_old = None
    for it in range(ITERS):
        rd = it + 1

        def first(m, carry, it=it):
            if it == 0:
                rr = load(r, m)
            else:
                dd, ss, xx, rr = update(it, m)
                save(r, m, rr)
                save(x, m, xx)
                save(d, m, dd)
                save(s, m, ss)
            zz = [u * v for u, v in zip(rr, load(invp, m))]
            save(z, m, zz)
            fill(m, zz)
            rz = [u * v for u, v in zip(rr, zz)]
            rho = (rz[0] + rz[3]) * 0.5 + (rz[1] + rz[2])
            rho = jnp.where(on_edge, rho * 0.5, rho)
            sums[0, pl.ds(m, 1), :] = jnp.sum(rho, axis=0, keepdims=True)
            f = load2(flux)
            fg = [f[a] * combo(SLOPES[a], zz) * scale_ref[m] for a in range(4)]
            ms = load2(mass)
            save(w, m, [ms[a] * zz[a] + combo(SLOPES[:, a], fg) for a in range(4)])
            return carry

        lax.fori_loop(0, modes, first, 0)
        multiply(grad_ref)

        def second(m, carry):
            g = gout[pl.ds(pl.multiple_of(m * rows, rows), rows), :]
            fg = flux[...] * g * scale_ref[m]
            fill(m, [fg])
            return carry

        lax.fori_loop(0, modes, second, 0)
        multiply(div_ref)

        def third(m, carry, rd=rd):
            zz = load(z, m)
            h = [u + gout[pl.ds(pl.multiple_of(m * rows + p * q, q), q), :]
                 for p, u in enumerate(load(w, m))]
            zh = zz[0] * h[0] + zz[1] * h[1] + zz[2] * h[2] + zz[3] * h[3]
            sums[1, pl.ds(m, 1), :] = jnp.sum(zh, axis=0, keepdims=True)
            return pack(rd, m, h, carry)

        lo, hi = lax.fori_loop(0, modes, third, (zero, zero))
        col_tx[rd, 0] = lo
        col_tx[rd, 1] = hi
        for k in range(2):
            part = jnp.sum(sums[k], axis=1, keepdims=True)
            line = jnp.sum(jnp.where(eye, part, 0.0), axis=0, keepdims=True)
            ar_tx[it, k:k + 1, :] = line
            ar_rx[it, 0, k:k + 1, :] = line
        for copy in halo_copies(rd):
            copy.start()

        def spread(offset, carry, it=it):
            pltpu.make_async_remote_copy(
                src_ref=ar_tx.at[it], dst_ref=ar_rx.at[it, offset],
                send_sem=atx_sem.at[it], recv_sem=arx_sem.at[it],
                device_id=place(offset), device_id_type=MESH).start()
            return carry

        lax.fori_loop(1, n, spread, 0)
        finish(rd, modes)
        gathered = ar_rx.at[it, pl.ds(1, n - 1)]
        pltpu.make_async_copy(gathered, gathered, arx_sem.at[it]).wait()
        total = jnp.sum(ar_rx[it], axis=0)
        rho, curve_sum = total[0:1] + pad, total[1:2] + pad
        if it == 0:
            mixing = jnp.zeros_like(rho)
            step_len = rho / curve_sum
        else:
            mixing = rho / rho_old
            step_len = rho / (curve_sum - mixing * rho / step_old)
        for k, line in enumerate((step_len, mixing)):
            tall = jnp.sum(jnp.where(eye, line, 0.0), axis=1, keepdims=True)
            coef[k] = jnp.broadcast_to(tall, (16, cols))
        rho_old, step_old = rho, step_len

    def stores(m):
        return [
            pltpu.make_async_copy(
                buf.at[c, m], out.at[m, :, pl.ds(c * LANES, LANES)], out_sem.at[k, c, m])
            for k, (buf, out) in enumerate(((sol_buf, sol_ref), (res_buf, res_ref)))
            for c in range(tiles)
        ]

    def last(m, carry):
        _, _, xx, rr = update(ITERS, m)
        for c in range(tiles):
            for p in range(4):
                cut = slice(c * LANES, (c + 1) * LANES)
                sol_buf[c, m, pl.ds(p, q, stride=4), :] = xx[p][:, cut]
                res_buf[c, m, pl.ds(p, q, stride=4), :] = rr[p][:, cut]
        for copy in stores(m):
            copy.start()
        return carry

    lax.fori_loop(0, modes, last, 0)

    for rd in range(ITERS + 1):
        for copy in halo_copies(rd):
            copy.wait_send()
    for it in range(ITERS):
        sent = ar_rx.at[it, pl.ds(1, n - 1)]
        pltpu.make_async_copy(sent, sent, atx_sem.at[it]).wait()

    def drain(m, carry):
        for copy in stores(m):
            copy.wait()
        return carry

    lax.fori_loop(0, modes, drain, 0)


def strided(refs, p, q):
    return jnp.concatenate([ref[pl.ds(p, q, stride=4), :] for ref in refs], axis=1)


def stack_table(table):
    top = table.astype(bf16)
    low = (table - top.astype(np.float32)).astype(bf16)
    return np.concatenate([top, top, low], axis=0)


def shards(nc, ns, forcing, metric, jacobian, mode_scale):
    modes, rows, cols = forcing.shape
    block = np.kron(np.eye(cols // 4), SLOPES).astype(np.float32)
    grad, div = stack_table(block.T), stack_table(block)
    n, q = nc * ns, rows // 4
    vm = pl.BlockSpec(memory_space=pltpu.VMEM)
    hbm = pl.BlockSpec(memory_space=pl.ANY)
    rounds = ITERS + 1
    tiles = cols // LANES
    split = pltpu.VMEM((tiles, modes, rows, LANES), f32)
    field = pltpu.VMEM((modes, rows, cols), f32)
    return pl.pallas_call(
        functools.partial(kernel, nc, ns, modes),
        out_shape=[jax.ShapeDtypeStruct(forcing.shape, f32)] * 2,
        in_specs=[pl.BlockSpec(memory_space=pltpu.SMEM)] + [hbm] * 3 + [vm] * 2,
        out_specs=[hbm, hbm],
        scratch_shapes=[
            field, field, field, field, field,
            pltpu.VMEM((modes + 2, rows, cols), f32),
            field,
            pltpu.VMEM((rows, cols), f32),
            pltpu.VMEM((rows, cols), f32),
            pltpu.VMEM((modes * rows, 2 * cols), bf16),
            pltpu.VMEM((modes * rows, cols), f32),
            pltpu.VMEM((2, 16, cols), f32),
            pltpu.VMEM((2, 16, cols), f32),
            pltpu.VMEM((rounds, 2, 16, cols), f32),
            pltpu.VMEM((rounds, 2, 16, cols), f32),
            pltpu.VMEM((rounds, 2, q, LANES), f32),
            pltpu.VMEM((rounds, 2, q, LANES), f32),
            pltpu.VMEM((rounds, 4, 1, LANES), f32),
            pltpu.VMEM((ITERS, 2, LANES), f32),
            pltpu.VMEM((ITERS, n, 2, LANES), f32),
            split,
            pltpu.VMEM((2, tiles, rows, LANES), f32),
            split, split,
            pltpu.SemaphoreType.DMA((rounds, 8)),
            pltpu.SemaphoreType.DMA((rounds, 8)),
            pltpu.SemaphoreType.DMA((ITERS,)),
            pltpu.SemaphoreType.DMA((ITERS,)),
            pltpu.SemaphoreType.DMA((3, tiles)),
            pltpu.SemaphoreType.DMA((2, tiles, modes)),
        ],
        compiler_params=pltpu.CompilerParams(
            collective_id=0, has_side_effects=True, vmem_limit_bytes=48 * 1024 * 1024),
    )(mode_scale, forcing, metric, jacobian, jnp.asarray(grad), jnp.asarray(div))


def solution(mesh):
    placed = (P(None, "curve", "sub"), P("curve", "sub"), P("curve", "sub"), P())
    return jax.shard_map(
        functools.partial(shards, mesh.shape["curve"], mesh.shape["sub"]),
        mesh=mesh,
        in_specs=placed,
        out_specs=(P(None, "curve", "sub"), P(None, "curve", "sub")),
        check_vma=False,
    )
```

profile of v0, /device:TPU:0, one launch (start us, length us, event | category | flops | bytes accessed | tf_op | source)
XLA Modules:
  0.0 57.5 jit_solution(636753857880626626)
XLA Ops:
  0.6 0.0 copy-start
  0.6 1.3 %copy-done = f32[12,96,256]{2,1,0:T(8,128)S(1)} copy-done((f32[12,96,256]{2,1,0:T(8,128)S(1)}, f32[12,96,256]{2,1,0:T(8,128)}, u32[]{:S(2)}) %copy-start) | copy-done | bytes 1179672
  1.9 0.0 copy-start.1
  1.9 1.0 %copy-done.1 = bf16[768,256]{1,0:T(8,128)(2,1)S(1)} copy-done((bf16[768,256]{1,0:T(8,128)(2,1)S(1)}, bf16[768,256]{1,0:T(8,128)(2,1)}, u32[]{:S(2)}) %copy-start.1) | copy-done | bytes 393240
  2.9 0.0 copy-start.2
  2.9 1.0 %copy-done.2 = bf16[768,256]{1,0:T(8,128)(2,1)S(1)} copy-done((bf16[768,256]{1,0:T(8,128)(2,1)S(1)}, bf16[768,256]{1,0:T(8,128)(2,1)}, u32[]{:S(2)}) %copy-start.2) | copy-done | bytes 393240
  3.9 0.0 copy-start.3
  3.9 0.9 %copy-done.3 = f32[96,256]{1,0:T(8,128)S(1)} copy-done((f32[96,256]{1,0:T(8,128)S(1)}, f32[96,256]{1,0:T(8,128)}, u32[]{:S(2)}) %copy-start.3) | copy-done | bytes 98328
  4.8 0.0 copy-start.4
  4.8 0.9 %copy-done.4 = f32[96,256]{1,0:T(8,128)S(1)} copy-done((f32[96,256]{1,0:T(8,128)S(1)}, f32[96,256]{1,0:T(8,128)}, u32[]{:S(2)}) %copy-start.4) | copy-done | bytes 98328
  5.7 0.0 copy-start.5
  5.7 0.7 %copy-done.5 = f32[12]{0:T(128)S(1)} copy-done((f32[12]{0:T(128)S(1)}, f32[12]{0:T(128)}, u32[]{:S(2)}) %copy-start.5) | copy-done | bytes 72
  6.3 49.2 %shard_map.77 = (f32[12,96,256]{2,1,0:T(8,128)S(1)}, f32[12,96,256]{2,1,0:T(8,128)S(1)}) custom-call(f32[12]{0:T(128)S(1)} %copy-done.5, f32[12,96,256]{2,1,0:T(8,128)S(1)} %copy-done, f32[96,256]{1,0:T(8,128)S(1)} %copy-done.3, f32[96,256]{1,0:T(8,128)S(1)} %copy-done.4, bf16[768,256]{1,0:T(8,128)(2,1)S(1)} %copy-done.2, bf16[768,256]{1,0:T(8,128)(2,1)S(1)} %copy-done.1), custom_call_target="tpu_custom_call" | custom-call | tf_op jit(solution)/shard_map/pallas_call | solution.py:380
  55.5 1.0 %copy.10 = f32[12,96,256]{2,1,0:T(8,128)} copy(f32[12,96,256]{2,1,0:T(8,128)S(1)} %get-tuple-element.4) | data formatting | bytes 2359296
  56.5 1.0 %copy.11 = f32[12,96,256]{2,1,0:T(8,128)} copy(f32[12,96,256]{2,1,0:T(8,128)S(1)} %get-tuple-element.5) | data formatting | bytes 2359296
Async XLA Ops:
  0.6 1.3 %copy-start = (f32[12,96,256]{2,1,0:T(8,128)S(1)}, f32[12,96,256]{2,1,0:T(8,128)}, u32[]{:S(2)}) copy-start(f32[12,96,256]{2,1,0:T(8,128)} %forcing_ref.1) | copy-start | bytes 3538948
  1.9 1.0 %copy-start.1 = (bf16[768,256]{1,0:T(8,128)(2,1)S(1)}, bf16[768,256]{1,0:T(8,128)(2,1)}, u32[]{:S(2)}) copy-start(bf16[768,256]{1,0:T(8,128)(2,1)} %constant.5.clone.div_ref) | copy-start | bytes 1179652
  2.9 1.0 %copy-start.2 = (bf16[768,256]{1,0:T(8,128)(2,1)S(1)}, bf16[768,256]{1,0:T(8,128)(2,1)}, u32[]{:S(2)}) copy-start(bf16[768,256]{1,0:T(8,128)(2,1)} %constant.4.clone.grad_ref) | copy-start | bytes 1179652
  3.9 0.9 %copy-start.3 = (f32[96,256]{1,0:T(8,128)S(1)}, f32[96,256]{1,0:T(8,128)}, u32[]{:S(2)}) copy-start(f32[96,256]{1,0:T(8,128)} %metric_ref.1) | copy-start | bytes 294916
  4.8 0.9 %copy-start.4 = (f32[96,256]{1,0:T(8,128)S(1)}, f32[96,256]{1,0:T(8,128)}, u32[]{:S(2)}) copy-start(f32[96,256]{1,0:T(8,128)} %jac_ref.1) | copy-start | bytes 294916
  5.7 0.7 %copy-start.5 = (f32[12]{0:T(128)S(1)}, f32[12]{0:T(128)}, u32[]{:S(2)}) copy-start(f32[12]{0:T(128)} %scale_ref.1) | copy-start | bytes 148
where the time goes:
time: 57.8 us; the launch traced here: 57.5 us
  Pallas kernels  49.2 us (85%)
  local copies, waits for them, and re-layouts  7.72 us (13%)
  between operations  0.65 us (1%)
    pallas_call x1, Pallas kernels, shards(): pl.pallas_call(functools.partial(kernel, nc, ns, modes), out_shape=[jax.S...  49.2 us
    unnamed x14, local copies, waits for them, and re-layouts  7.72 us

commit v1 on v0

v1 whole, which is shorter than its diff:
```python
import functools
import math

import jax
import jax.numpy as jnp
import numpy as np
from jax import lax
from jax.experimental import pallas as pl
from jax.experimental.pallas import tpu as pltpu
from jax.sharding import PartitionSpec as P

ITERS = 3
GROUPS = 2
UNROLL = 2
MESH = pl.DeviceIdType.MESH
LANES = 128
f32 = jnp.float32
bf16 = jnp.bfloat16


def gll_tables():
    points = np.array([-1.0, -1.0 / math.sqrt(5.0), 1.0 / math.sqrt(5.0), 1.0])
    weights = np.array([1.0 / 6.0, 5.0 / 6.0, 5.0 / 6.0, 1.0 / 6.0])
    factor = np.array(
        [np.prod([points[j] - points[m] for m in range(4) if m != j]) for j in range(4)]
    )
    slopes = np.zeros((4, 4))
    for i in range(4):
        for j in range(4):
            if i != j:
                slopes[i, j] = factor[i] / (factor[j] * (points[i] - points[j]))
        slopes[i, i] = sum((1.0 / (points[i] - points[m]) for m in range(4) if m != i))
    return (slopes, weights)


SLOPES, WEIGHTS = gll_tables()


def combo(coefs, parts):
    total = None
    for c, v in zip(coefs, parts):
        if abs(c) < 1e-12:
            continue
        term = v * f32(c)
        total = term if total is None else total + term
    return total


def kernel(
    nc, ns, modes, groups,
    scale_hbm, forcing_ref, metric_ref, jac_ref, grad_hbm, div_hbm,
    x, r,
    z, d, s, w, invp, mass, flux, zcat, gout, sums, coef,
    row_tx, row_rx, col_tx, col_rx, cor_rx, ar_tx, ar_rx,
    source, factors, grad_ref, div_ref, scale_ref,
    htx_sem, hrx_sem, atx_sem, arx_sem, in_sem, table_sem,
):
    rows, cols = metric_ref.shape
    q = rows // 4
    n = nc * ns
    half = cols - LANES
    tiles = cols // LANES
    per = modes // groups
    slots = row_tx.shape[2]
    loads, sources = [], []
    for c in range(tiles):
        cut = pl.ds(c * LANES, LANES)
        loads += [
            pltpu.make_async_copy(jac_ref.at[:, cut], factors.at[0, c], in_sem.at[0, c]),
            pltpu.make_async_copy(metric_ref.at[:, cut], factors.at[1, c], in_sem.at[1, c]),
        ]
        sources.append(
            pltpu.make_async_copy(forcing_ref.at[:, :, cut], source.at[c], in_sem.at[2, c]))
    div_load = pltpu.make_async_copy(div_hbm, div_ref, table_sem.at[0])
    grad_load = pltpu.make_async_copy(grad_hbm, grad_ref, table_sem.at[1])
    scale_load = pltpu.make_async_copy(scale_hbm, scale_ref, table_sem.at[2])
    for copy in loads + sources + [div_load, scale_load, grad_load]:
        copy.start()

    me_c, me_s = lax.axis_index("curve"), lax.axis_index("sub")
    me = me_c * ns + me_s
    up, down = lax.rem(me_c + nc - 1, nc), lax.rem(me_c + 1, nc)
    left, right = lax.rem(me_s + ns - 1, ns), lax.rem(me_s + 1, ns)

    def place(offset):
        target = lax.rem(me + offset, n)
        return (target // ns, lax.rem(target, ns))

    barrier = pltpu.get_barrier_semaphore()

    def greet(offset, carry):
        pl.semaphore_signal(barrier, inc=1, device_id=place(offset), device_id_type=MESH)
        return carry

    lax.fori_loop(1, n, greet, 0)

    lane_full = lax.broadcasted_iota(jnp.int32, (q, cols), 1)
    lane = lax.broadcasted_iota(jnp.int32, (q, LANES), 1)
    row_at = lax.broadcasted_iota(jnp.int32, (q, cols), 0)
    phase = lane_full % 4
    on_edge = (phase == 0) | (phase == 3)
    take_next = (phase == 3) & (lane_full != cols - 1)
    take_prev = (phase == 0) & (lane_full != 0)

    def load(ref, m):
        return [ref[m, p * q:(p + 1) * q, :] for p in range(4)]

    def save(ref, m, parts):
        for p in range(4):
            ref[m, p * q:(p + 1) * q, :] = parts[p]

    def load2(ref):
        return [ref[p * q:(p + 1) * q, :] for p in range(4)]

    def pack(k, m, slot, h, tops):
        lo, hi = tops
        row_tx[k, 0, pl.ds(slot, 1), :] = h[0][0:1, :]
        row_tx[k, 1, pl.ds(slot, 1), :] = h[3][q - 1:q, :]
        t0 = h[0] + jnp.where(row_at == 0, 0.0, pltpu.roll(h[3], 1, 0))
        t3 = h[3] + jnp.where(row_at == q - 1, 0.0, pltpu.roll(h[0], q - 1, 0))
        t = [t0, h[1], h[2], t3]
        save(w, m, t)
        for p in range(4):
            at = 4 * slot + p
            lo = jnp.where(lane == at, pltpu.roll(t[p][:, :LANES], at, 1), lo)
            hi = jnp.where(lane == at, pltpu.roll(t[p][:, half:], at + 1, 1), hi)
        return lo, hi

    def halo_copies(k):
        plan = [
            (col_tx.at[k, 0, pl.ds(0, 1)], cor_rx.at[k, 3], (up, left)),
            (col_tx.at[k, 1, pl.ds(0, 1)], cor_rx.at[k, 2], (up, right)),
            (col_tx.at[k, 0, pl.ds(q - 1, 1)], cor_rx.at[k, 1], (down, left)),
            (col_tx.at[k, 1, pl.ds(q - 1, 1)], cor_rx.at[k, 0], (down, right)),
            (row_tx.at[k, 0], row_rx.at[k, 1], (up, me_s)),
            (row_tx.at[k, 1], row_rx.at[k, 0], (down, me_s)),
            (col_tx.at[k, 0], col_rx.at[k, 1], (me_c, left)),
            (col_tx.at[k, 1], col_rx.at[k, 0], (me_c, right)),
        ]
        return [
            pltpu.make_async_remote_copy(
                src_ref=src, dst_ref=dst, send_sem=htx_sem.at[k, e], recv_sem=hrx_sem.at[k, e],
                device_id=where, device_id_type=MESH)
            for e, (src, dst, where) in enumerate(plan)
        ]

    def send(k, tops):
        col_tx[k, 0], col_tx[k, 1] = tops
        for copy in halo_copies(k):
            copy.start()

    def arrive(k):
        for copy in halo_copies(k):
            copy.wait_recv()
        ph = lax.broadcasted_iota(jnp.int32, (1, LANES), 1) % 4
        edge_row = lax.broadcasted_iota(jnp.int32, (q, LANES), 0)
        merged = []
        for side in range(2):
            above, below = cor_rx[k, side], cor_rx[k, 2 + side]
            above = jnp.where(ph == 0, pltpu.roll(above, LANES - 3, 1), 0.0)
            below = jnp.where(ph == 3, pltpu.roll(below, 3, 1), 0.0)
            c = col_rx[k, side]
            c = c + jnp.where(edge_row == 0, above, 0.0) + jnp.where(edge_row == q - 1, below, 0.0)
            merged.append(c)
        return merged

    def assembled(k, m, slot, merged):
        t = load(w, m)
        t[0] = t[0] + jnp.where(row_at == 0, row_rx[k, 0, pl.ds(slot, 1), :], 0.0)
        t[3] = t[3] + jnp.where(row_at == q - 1, row_rx[k, 1, pl.ds(slot, 1), :], 0.0)
        out = []
        for p in range(4):
            at = 4 * slot + p
            c = t[p] + jnp.where(
                take_next, pltpu.roll(t[p], cols - 1, 1),
                jnp.where(take_prev, pltpu.roll(t[p], 1, 1), 0.0))
            a = jnp.where(lane == 0, pltpu.roll(merged[0], LANES - at, 1), 0.0)
            b = jnp.where(lane == LANES - 1, pltpu.roll(merged[1], LANES - 1 - at, 1), 0.0)
            pieces = [c[:, e * LANES:(e + 1) * LANES] for e in range(tiles)]
            pieces[0] = pieces[0] + a
            pieces[-1] = pieces[-1] + b
            out.append(jnp.concatenate(pieces, axis=1))
        return out

    edge_w, mid_w = f32(1.0 / 6.0), f32(5.0 / 6.0)
    col_w = jnp.where(on_edge, edge_w, mid_w)
    mw, fw = [], []
    for copy in loads:
        copy.wait()
    for p in range(4):
        grid_w = col_w * (edge_w if p in (0, 3) else mid_w)
        mw.append(strided([factors.at[0, c] for c in range(tiles)], p, q) * grid_w)
        fw.append(strided([factors.at[1, c] for c in range(tiles)], p, q) * grid_w)
        mass[p * q:(p + 1) * q, :] = mw[p]
        flux[p * q:(p + 1) * q, :] = fw[p]
    zero = jnp.zeros((q, LANES), f32)
    tops = pack(0, modes, per, mw, (zero, zero))
    div_load.wait()
    table = div_ref[:cols, :].astype(f32) + div_ref[2 * cols:, :].astype(f32)
    by_cols = jnp.dot(flux[...], table * table, precision=lax.Precision.HIGHEST,
                      preferred_element_type=f32)
    squared = SLOPES * SLOPES
    lap = [combo(squared[:, a], fw) + by_cols[a * q:(a + 1) * q, :] for a in range(4)]
    tops = pack(0, modes + 1, per + 1, lap, tops)
    for copy in sources:
        copy.wait()
    for g in range(groups):

        def start_body(slot, carry, g=g):
            m = g * per + slot
            h = [strided([source.at[c, m] for c in range(tiles)], p, q)
                 * mass[p * q:(p + 1) * q, :] for p in range(4)]
            return pack(g, m, slot, h, carry)

        tops = lax.fori_loop(0, per, start_body, tops if g == 0 else (zero, zero), unroll=UNROLL)
        if g == 0:
            pl.semaphore_wait(barrier, n - 1)
        send(g, tops)
    scale_load.wait()
    grad_load.wait()

    pad = (lax.broadcasted_iota(jnp.int32, (1, LANES), 1) >= per).astype(f32)
    eye = lax.broadcasted_iota(jnp.int32, (slots, LANES), 0) == lax.broadcasted_iota(
        jnp.int32, (slots, LANES), 1)

    def update(it, g, m, slot, ww):
        a, b = coef[g, 0, pl.ds(slot, 1), :], coef[g, 1, pl.ds(slot, 1), :]
        zz = load(z, m)
        if it > 1:
            dd, ss = load(d, m), load(s, m)
            zz = [u + b * v for u, v in zip(zz, dd)]
            ww = [u + b * v for u, v in zip(ww, ss)]
            xx = [u + a * v for u, v in zip(load(x, m), zz)]
        else:
            xx = [a * v for v in zz]
        rr = [u - a * v for u, v in zip(load(r, m), ww)]
        return zz, ww, xx, rr

    def fill(slot, parts):
        v = jnp.concatenate(parts, axis=0)
        top = v.astype(bf16)
        at = pl.ds(pl.multiple_of(slot * rows, rows), rows)
        zcat[at, :cols] = top
        zcat[at, cols:] = (v - top.astype(f32)).astype(bf16)

    def multiply(table_ref):
        gout[...] = (
            jnp.dot(zcat[...], table_ref[:2 * cols, :], preferred_element_type=f32)
            + jnp.dot(zcat[:, :cols], table_ref[2 * cols:, :], preferred_element_type=f32))

    old = [None] * groups

    def coefficients(it, g):
        k = it * groups + g
        gathered = ar_rx.at[k, pl.ds(1, n - 1)]
        pltpu.make_async_copy(gathered, gathered, arx_sem.at[k]).wait()
        total = jnp.sum(ar_rx[k], axis=0)
        rho, curve_sum = total[0:1] + pad, total[1:2] + pad
        if it == 0:
            mixing = jnp.zeros_like(rho)
            step_len = rho / curve_sum
        else:
            mixing = rho / old[g][0]
            step_len = rho / (curve_sum - mixing * rho / old[g][1])
        for e, line in enumerate((step_len, mixing)):
            tall = jnp.sum(jnp.where(eye, line, 0.0), axis=1, keepdims=True)
            coef[g, e] = jnp.broadcast_to(tall, (slots, cols))
        old[g] = (rho, step_len)

    for it in range(ITERS):
        for g in range(groups):
            base = g * per
            k = it * groups + g
            merged = arrive(k)
            if it == 0 and g == 0:
                for e in range(2):
                    save(w, modes + e, assembled(k, modes + e, per + e, merged))
            if it > 0:
                coefficients(it - 1, g)

            def first(slot, carry, it=it, g=g, k=k, base=base, merged=merged):
                m = base + slot
                ww = assembled(k, m, slot, merged)
                if it == 0:
                    rr = ww
                    inv = [1.0 / (u + scale_ref[m] * v)
                           for u, v in zip(load(w, modes), load(w, modes + 1))]
                    save(invp, m, inv)
                else:
                    dd, ss, xx, rr = update(it, g, m, slot, ww)
                    save(x, m, xx)
                    save(d, m, dd)
                    save(s, m, ss)
                    inv = load(invp, m)
                save(r, m, rr)
                zz = [u * v for u, v in zip(rr, inv)]
                save(z, m, zz)
                fill(slot, zz)
                rz = [u * v for u, v in zip(rr, zz)]
                rho = (rz[0] + rz[3]) * 0.5 + (rz[1] + rz[2])
                rho = jnp.where(on_edge, rho * 0.5, rho)
                sums[0, pl.ds(slot, 1), :] = jnp.sum(rho, axis=0, keepdims=True)
                f = load2(flux)
                fg = [f[a] * combo(SLOPES[a], zz) * scale_ref[m] for a in range(4)]
                ms = load2(mass)
                save(w, m, [ms[a] * zz[a] + combo(SLOPES[:, a], fg) for a in range(4)])
                return carry

            lax.fori_loop(0, per, first, 0, unroll=UNROLL)
            multiply(grad_ref)

            def second(slot, carry, base=base):
                grad = gout[pl.ds(pl.multiple_of(slot * rows, rows), rows), :]
                fill(slot, [flux[...] * grad * scale_ref[base + slot]])
                return carry

            lax.fori_loop(0, per, second, 0, unroll=UNROLL)
            multiply(div_ref)

            def third(slot, carry, k=k, base=base):
                m = base + slot
                zz = load(z, m)
                h = [u + gout[pl.ds(pl.multiple_of(slot * rows + p * q, q), q), :]
                     for p, u in enumerate(load(w, m))]
                zh = zz[0] * h[0] + zz[1] * h[1] + zz[2] * h[2] + zz[3] * h[3]
                sums[1, pl.ds(slot, 1), :] = jnp.sum(zh, axis=0, keepdims=True)
                return pack(k + groups, m, slot, h, carry)

            tops = lax.fori_loop(0, per, third, (zero, zero), unroll=UNROLL)
            send(k + groups, tops)
            for e in range(2):
                part = jnp.sum(sums[e], axis=1, keepdims=True)
                line = jnp.sum(jnp.where(eye, part, 0.0), axis=0, keepdims=True)
                ar_tx[k, e:e + 1, :] = line
                ar_rx[k, 0, e:e + 1, :] = line

            def spread(offset, carry, k=k):
                pltpu.make_async_remote_copy(
                    src_ref=ar_tx.at[k], dst_ref=ar_rx.at[k, offset],
                    send_sem=atx_sem.at[k], recv_sem=arx_sem.at[k],
                    device_id=place(offset), device_id_type=MESH).start()
                return carry

            lax.fori_loop(1, n, spread, 0)

    for g in range(groups):
        k = ITERS * groups + g
        merged = arrive(k)
        coefficients(ITERS - 1, g)

        def last(slot, carry, g=g, k=k, merged=merged):
            m = g * per + slot
            _, _, xx, rr = update(ITERS, g, m, slot, assembled(k, m, slot, merged))
            save(x, m, xx)
            save(r, m, rr)
            return carry

        lax.fori_loop(0, per, last, 0, unroll=UNROLL)

    for k in range((ITERS + 1) * groups):
        for copy in halo_copies(k):
            copy.wait_send()
    for k in range(ITERS * groups):
        sent = ar_rx.at[k, pl.ds(1, n - 1)]
        pltpu.make_async_copy(sent, sent, atx_sem.at[k]).wait()


def node_order(x, r, sol_ref, res_ref, sol_buf, res_buf, sem):
    modes, rows, cols = x.shape
    q, tiles = rows // 4, cols // LANES

    def stores(m):
        return [
            pltpu.make_async_copy(
                buf.at[c, m], out.at[m, :, pl.ds(c * LANES, LANES)], sem.at[k, c, m])
            for k, (buf, out) in enumerate(((sol_buf, sol_ref), (res_buf, res_ref)))
            for c in range(tiles)
        ]

    def body(m, carry):
        for c in range(tiles):
            for p in range(4):
                cut = slice(c * LANES, (c + 1) * LANES)
                sol_buf[c, m, pl.ds(p, q, stride=4), :] = x[m, p * q:(p + 1) * q, cut]
                res_buf[c, m, pl.ds(p, q, stride=4), :] = r[m, p * q:(p + 1) * q, cut]
        for copy in stores(m):
            copy.start()
        return carry

    lax.fori_loop(0, modes, body, 0)

    def drain(m, carry):
        for copy in stores(m):
            copy.wait()
        return carry

    lax.fori_loop(0, modes, drain, 0)


def strided(refs, p, q):
    return jnp.concatenate([ref[pl.ds(p, q, stride=4), :] for ref in refs], axis=1)


def stack_table(table):
    top = table.astype(bf16)
    low = (table - top.astype(np.float32)).astype(bf16)
    return np.concatenate([top, top, low], axis=0)


def shards(nc, ns, forcing, metric, jacobian, mode_scale):
    modes, rows, cols = forcing.shape
    block = np.kron(np.eye(cols // 4), SLOPES).astype(np.float32)
    grad, div = stack_table(block.T), stack_table(block)
    n, q, tiles = nc * ns, rows // 4, cols // LANES
    groups = GROUPS if modes % GROUPS == 0 else 1
    per = modes // groups
    slots = -(-(per + 2) // 8) * 8
    vm = pl.BlockSpec(memory_space=pltpu.VMEM)
    hbm = pl.BlockSpec(memory_space=pltpu.HBM)
    rounds, sums = (ITERS + 1) * groups, ITERS * groups
    field = pltpu.VMEM((modes, rows, cols), f32)
    split = pltpu.VMEM((tiles, modes, rows, LANES), f32)
    table = pltpu.VMEM(grad.shape, bf16)
    shape = jax.ShapeDtypeStruct(forcing.shape, f32)
    x, r = pl.pallas_call(
        functools.partial(kernel, nc, ns, modes, groups),
        out_shape=[shape] * 2,
        in_specs=[hbm] * 6,
        out_specs=[vm, vm],
        scratch_shapes=[
            field, field, field,
            pltpu.VMEM((modes + 2, rows, cols), f32),
            field,
            pltpu.VMEM((rows, cols), f32),
            pltpu.VMEM((rows, cols), f32),
            pltpu.VMEM((per * rows, 2 * cols), bf16),
            pltpu.VMEM((per * rows, cols), f32),
            pltpu.VMEM((2, slots, cols), f32),
            pltpu.VMEM((groups, 2, slots, cols), f32),
            pltpu.VMEM((rounds, 2, slots, cols), f32),
            pltpu.VMEM((rounds, 2, slots, cols), f32),
            pltpu.VMEM((rounds, 2, q, LANES), f32),
            pltpu.VMEM((rounds, 2, q, LANES), f32),
            pltpu.VMEM((rounds, 4, 1, LANES), f32),
            pltpu.VMEM((sums, 2, LANES), f32),
            pltpu.VMEM((sums, n, 2, LANES), f32),
            split,
            pltpu.VMEM((2, tiles, rows, LANES), f32),
            table, table,
            pltpu.SMEM((modes,), f32),
            pltpu.SemaphoreType.DMA((rounds, 8)),
            pltpu.SemaphoreType.DMA((rounds, 8)),
            pltpu.SemaphoreType.DMA((sums,)),
            pltpu.SemaphoreType.DMA((sums,)),
            pltpu.SemaphoreType.DMA((3, tiles)),
            pltpu.SemaphoreType.DMA((3,)),
        ],
        compiler_params=pltpu.CompilerParams(
            collective_id=0, has_side_effects=True, vmem_limit_bytes=63000000),
    )(mode_scale, forcing, metric, jacobian, jnp.asarray(grad), jnp.asarray(div))
    return pl.pallas_call(
        node_order,
        out_shape=[shape] * 2,
        in_specs=[vm, vm],
        out_specs=[hbm, hbm],
        scratch_shapes=[split, split, pltpu.SemaphoreType.DMA((2, tiles, modes))],
        compiler_params=pltpu.CompilerParams(vmem_limit_bytes=16 * 1024 * 1024),
    )(x, r)


def solution(mesh):
    placed = (P(None, "curve", "sub"), P("curve", "sub"), P("curve", "sub"), P())
    return jax.shard_map(
        functools.partial(shards, mesh.shape["curve"], mesh.shape["sub"]),
        mesh=mesh,
        in_specs=placed,
        out_specs=(P(None, "curve", "sub"), P(None, "curve", "sub")),
        check_vma=False,
    )
```

time: 57.8 us -> 45.9 us (0.79)
  Pallas kernels: 49.2 us -> 42.5 us
  local copies, waits for them, and re-layouts: 7.72 us -> 2.53 us
    pallas_call x1 -> x2, Pallas kernels: 49.2 us -> 42.5 us  [the longest x1 40.7 us: shards(): pl.pallas_call(functools.partial(kernel, nc, ns, modes, groups), out_shap...]
    unnamed x14 -> x4, local copies, waits for them, and re-layouts: 7.72 us -> 2.53 us
where the time goes in v1:
time: 45.9 us; the launch traced here: 45.7 us
  Pallas kernels  42.5 us (93%)
  local copies, waits for them, and re-layouts  2.53 us (6%)
  between operations  0.65 us (1%)
    pallas_call x1, Pallas kernels, shards(): pl.pallas_call(functools.partial(kernel, nc, ns, modes, groups), out_shap...  40.7 us
    unnamed x4, local copies, waits for them, and re-layouts  2.53 us
    pallas_call x1, Pallas kernels, shards(): pl.pallas_call(node_order, out_shape=[shape] * 2, in_specs=[vm, vm], out_...  1.8 us

profile of v1, /device:TPU:0, one launch (start us, length us, event | category | flops | bytes accessed | tf_op | source)
XLA Modules:
  0.0 45.7 jit_solution(3485154048365778395)
XLA Ops:
  0.6 40.7 %shard_map.77 = (f32[12,96,256]{2,1,0:T(8,128)}, f32[12,96,256]{2,1,0:T(8,128)}) custom-call(f32[12]{0:T(128)} %scale_hbm.1, f32[12,96,256]{2,1,0:T(8,128)} %forcing_ref.1, f32[96,256]{1,0:T(8,128)} %metric_ref.1, f32[96,256]{1,0:T(8,128)} %jac_ref.1, bf16[768,256]{1,0:T(8,128)(2,1)} %constant.4.clone.grad_hbm, bf16[768,256]{1,0:T(8,128)(2,1)} %constant.5.clone.div_hbm), custom_call_target="tpu_custom_call" | custom-call | tf_op jit(solution)/shard_map/pallas_call | solution.py:425
  41.3 0.0 copy-start
  41.3 1.3 %copy-done = f32[12,96,256]{2,1,0:T(8,128)S(1)} copy-done((f32[12,96,256]{2,1,0:T(8,128)S(1)}, f32[12,96,256]{2,1,0:T(8,128)}, u32[]{:S(2)}) %copy-start) | copy-done | bytes 1179672
  42.6 0.0 copy-start.1
  42.6 1.3 %copy-done.1 = f32[12,96,256]{2,1,0:T(8,128)S(1)} copy-done((f32[12,96,256]{2,1,0:T(8,128)S(1)}, f32[12,96,256]{2,1,0:T(8,128)}, u32[]{:S(2)}) %copy-start.1) | copy-done | bytes 1179672
  43.9 1.8 %shard_map.78 = (f32[12,96,256]{2,1,0:T(8,128)}, f32[12,96,256]{2,1,0:T(8,128)}) custom-call(f32[12,96,256]{2,1,0:T(8,128)S(1)} %copy-done, f32[12,96,256]{2,1,0:T(8,128)S(1)} %copy-done.1), custom_call_target="tpu_custom_call" | custom-call | tf_op jit(solution)/shard_map/pallas_call | solution.py:461
Async XLA Ops:
  41.3 1.3 %copy-start = (f32[12,96,256]{2,1,0:T(8,128)S(1)}, f32[12,96,256]{2,1,0:T(8,128)}, u32[]{:S(2)}) copy-start(f32[12,96,256]{2,1,0:T(8,128)} %get-tuple-element.4.x) | copy-start | bytes 3538948
  42.6 1.3 %copy-start.1 = (f32[12,96,256]{2,1,0:T(8,128)S(1)}, f32[12,96,256]{2,1,0:T(8,128)}, u32[]{:S(2)}) copy-start(f32[12,96,256]{2,1,0:T(8,128)} %get-tuple-element.5.r) | copy-start | bytes 3538948

commit v2 on v1

--- a/solution.py
+++ b/solution.py
@@ -11,7 +11,7 @@
 
 ITERS = 3
 GROUPS = 2
-UNROLL = 2
+UNROLL = True
 MESH = pl.DeviceIdType.MESH
 LANES = 128
 f32 = jnp.float32
@@ -456,8 +456,8 @@
             pltpu.SemaphoreType.DMA((3,)),
         ],
         compiler_params=pltpu.CompilerParams(
-            collective_id=0, has_side_effects=True, vmem_limit_bytes=63000000),
-    )(mode_scale, forcing, metric, jacobian, jnp.asarray(grad), jnp.asarray(div))
+            collective_id=0, has_side_effects=True, vmem_limit_bytes=41943040),
+    )(*[pltpu.with_memory_space_constraint(v, pltpu.HBM) for v in (mode_scale, forcing, metric, jacobian, jnp.asarray(grad), jnp.asarray(div))])
     return pl.pallas_call(
         node_order,
         out_shape=[shape] * 2,

time: 45.9 us -> 36.5 us (0.80)
  Pallas kernels: 42.5 us -> 35.7 us
  local copies, waits for them, and re-layouts: 2.53 us -> 0 us
    pallas_call x1, Pallas kernels: 40.7 us -> 33.9 us  [shards(): pl.pallas_call(functools.partial(kernel, nc, ns, modes, groups), out_shap...]
    unnamed x4 -> x0, local copies, waits for them, and re-layouts: 2.53 us -> none
where the time goes in v2:
time: 36.5 us; the launch traced here: 36.3 us
  Pallas kernels  35.7 us (98%)
  between operations  0.64 us (2%)
    pallas_call x1, Pallas kernels, shards(): pl.pallas_call(functools.partial(kernel, nc, ns, modes, groups), out_shap...  33.9 us
    pallas_call x1, Pallas kernels, shards(): pl.pallas_call(node_order, out_shape=[shape] * 2, in_specs=[vm, vm], out_...  1.8 us

profile of v2, /device:TPU:0, one launch (start us, length us, event | category | flops | bytes accessed | tf_op | source)
XLA Modules:
  0.0 36.3 jit_solution(12138087989677492564)
XLA Ops:
  0.6 33.9 %shard_map.77 = (f32[12,96,256]{2,1,0:T(8,128)S(1)}, f32[12,96,256]{2,1,0:T(8,128)S(1)}) custom-call(f32[12]{0:T(128)} %scale_hbm.1, f32[12,96,256]{2,1,0:T(8,128)} %forcing_ref.1, f32[96,256]{1,0:T(8,128)} %metric_ref.1, f32[96,256]{1,0:T(8,128)} %jac_ref.1, bf16[768,256]{1,0:T(8,128)(2,1)} %constant.4.clone.grad_hbm, bf16[768,256]{1,0:T(8,128)(2,1)} %constant.5.clone.div_hbm), custom_call_target="tpu_custom_call" | custom-call | tf_op jit(solution)/shard_map/pallas_call | solution.py:425
  34.5 1.8 %shard_map.78 = (f32[12,96,256]{2,1,0:T(8,128)}, f32[12,96,256]{2,1,0:T(8,128)}) custom-call(f32[12,96,256]{2,1,0:T(8,128)S(1)} %get-tuple-element.4.x, f32[12,96,256]{2,1,0:T(8,128)S(1)} %get-tuple-element.5.r), custom_call_target="tpu_custom_call" | custom-call | tf_op jit(solution)/shard_map/pallas_call | solution.py:461

commit v3 on v2

--- a/solution.py
+++ b/solution.py
@@ -128,12 +128,12 @@
 
     def halo_copies(k):
         plan = [
+            (row_tx.at[k, 0], row_rx.at[k, 1], (up, me_s)),
+            (row_tx.at[k, 1], row_rx.at[k, 0], (down, me_s)),
             (col_tx.at[k, 0, pl.ds(0, 1)], cor_rx.at[k, 3], (up, left)),
             (col_tx.at[k, 1, pl.ds(0, 1)], cor_rx.at[k, 2], (up, right)),
             (col_tx.at[k, 0, pl.ds(q - 1, 1)], cor_rx.at[k, 1], (down, left)),
             (col_tx.at[k, 1, pl.ds(q - 1, 1)], cor_rx.at[k, 0], (down, right)),
-            (row_tx.at[k, 0], row_rx.at[k, 1], (up, me_s)),
-            (row_tx.at[k, 1], row_rx.at[k, 0], (down, me_s)),
             (col_tx.at[k, 0], col_rx.at[k, 1], (me_c, left)),
             (col_tx.at[k, 1], col_rx.at[k, 0], (me_c, right)),
         ]
@@ -341,7 +341,7 @@
                     device_id=place(offset), device_id_type=MESH).start()
                 return carry
 
-            lax.fori_loop(1, n, spread, 0)
+            lax.fori_loop(1, n, spread, 0, unroll=True if n <= 32 else 1)
 
     for g in range(groups):
         k = ITERS * groups + g

time: 36.5 us -> 35.9 us (0.984)
  Pallas kernels: 35.7 us -> 35.1 us
    pallas_call x1, Pallas kernels: 33.9 us -> 33.3 us  [shards(): pl.pallas_call(functools.partial(kernel, nc, ns, modes, groups), out_shap...]
where the time goes in v3:
time: 35.9 us; the launch traced here: 35.7 us
  Pallas kernels  35.1 us (98%)
  between operations  0.64 us (2%)
    pallas_call x1, Pallas kernels, shards(): pl.pallas_call(functools.partial(kernel, nc, ns, modes, groups), out_shap...  33.3 us
    pallas_call x1, Pallas kernels, shards(): pl.pallas_call(node_order, out_shape=[shape] * 2, in_specs=[vm, vm], out_...  1.8 us

profile of v3, /device:TPU:0, one launch (start us, length us, event | category | flops | bytes accessed | tf_op | source)
XLA Modules:
  0.0 35.7 jit_solution(5842819093337775669)
XLA Ops:
  0.6 33.3 %shard_map.77 = (f32[12,96,256]{2,1,0:T(8,128)S(1)}, f32[12,96,256]{2,1,0:T(8,128)S(1)}) custom-call(f32[12]{0:T(128)} %scale_hbm.1, f32[12,96,256]{2,1,0:T(8,128)} %forcing_ref.1, f32[96,256]{1,0:T(8,128)} %metric_ref.1, f32[96,256]{1,0:T(8,128)} %jac_ref.1, bf16[768,256]{1,0:T(8,128)(2,1)} %constant.4.clone.grad_hbm, bf16[768,256]{1,0:T(8,128)(2,1)} %constant.5.clone.div_hbm), custom_call_target="tpu_custom_call" | custom-call | tf_op jit(solution)/shard_map/pallas_call | solution.py:425
  33.9 1.8 %shard_map.78 = (f32[12,96,256]{2,1,0:T(8,128)}, f32[12,96,256]{2,1,0:T(8,128)}) custom-call(f32[12,96,256]{2,1,0:T(8,128)S(1)} %get-tuple-element.4.x, f32[12,96,256]{2,1,0:T(8,128)S(1)} %get-tuple-element.5.r), custom_call_target="tpu_custom_call" | custom-call | tf_op jit(solution)/shard_map/pallas_call | solution.py:461
